TPU v7x, 32 devices: a whole 2x2x4 slice. The times are simulated.
32 devices in a mesh: col: 4 (over z), row: 8 (over y, x, core).
Axes of the slice: x: 2, y: 2, z: 4, core: 2. Of those that a mesh axis runs over, the one named last changes fastest.
Arguments:
- trans_mat: bfloat16 [24576, 24576], P('row', 'col')
- x_start: float32 [24576, 256], P(('col', 'row'))
- teleport: float32 [24576, 256], P(('col', 'row'))
- dangling: int32 [24576], P(('col', 'row'))
Outputs:
- output: float32 [24576, 256], P(('col', 'row'))
All inputs are finite; a program needn't handle non-finite values.
Results may differ from a plain program's by a relative error of at most 0.001.
Values are sent between devices in bfloat16 or wider.
A program may use at most 1 GiB of HBM per device.

v0:
```python
import jax
import jax.numpy as jnp
from jax import lax
from jax.sharding import PartitionSpec as P

SWEEPS = 8
DAMPING = 0.85


def solution(mesh):
    row_size = mesh.shape['row']
    col_size = mesh.shape['col']
    realign = [(col_idx * row_size + row_idx, row_idx * col_size + col_idx)
               for row_idx in range(row_size) for col_idx in range(col_size)]

    def local_sweeps(mat_tile, x_piece, tele_piece, dang_piece):
        vertex_count = mat_tile.shape[1] * col_size
        dang_col = dang_piece.astype(jnp.float32)[:, None]
        x_cur = x_piece
        for sweep_idx in range(SWEEPS):
            dang_mass = lax.psum(jnp.sum(dang_col * x_cur, axis=0), ('col', 'row')) / vertex_count
            x_src = lax.all_gather(x_cur.astype(jnp.bfloat16), 'row', axis=0, tiled=True)
            part_prod = jnp.dot(mat_tile, x_src, preferred_element_type=jnp.float32)
            folded = lax.psum_scatter(part_prod, 'col', scatter_dimension=0, tiled=True)
            aligned = lax.ppermute(folded, ('col', 'row'), perm=realign)
            x_cur = DAMPING * aligned + (DAMPING * dang_mass + (1.0 - DAMPING))[None, :] * tele_piece
        return x_cur

    vec_spec = P(('col', 'row'), None)
    return jax.shard_map(local_sweeps, mesh=mesh,
                         in_specs=(P('row', 'col'), vec_spec, vec_spec, P(('col', 'row'))),
                         out_specs=vec_spec, check_vma=False)
```

profile of v0, /device:TPU:0, one launch (start us, length us, event | category | flops | bytes accessed | tf_op | source)
XLA Modules:
  0.0 1516.8 jit_solution(15339457513417300680)
XLA Ops:
  7.2 2.3 fusion.7
  9.6 34.8 %all-gather.9.cloned.1.call-done = bf16[6144,256]{1,0:T(8,128)(2,1)} async-done(((bf16[768,256]{1,0:T(8,128)(2,1)}), bf16[6144,256]{1,0:T(8,128)(2,1)}) %all-gather.9.cloned.1.call-update) | async-done | bytes 3145744 | tf_op jit(solution)/shard_map/all_gather | solution.py:22
  44.4 19.0 %fusion.8 = f32[3072,256]{1,0:T(8,128)} fusion(bf16[3072,6144]{1,0:T(8,128)(2,1)} %param.4, bf16[6144,256]{1,0:T(8,128)(2,1)} %all-gather.9.cloned.1.call-done), kind=kOutput, calls=%fused_computation.39 | convolution fusion | flops 9663676416 | bytes 44040192 | tf_op jit(solution)/shard_map/dot_general | solution.py:23
  63.5 60.6 %reduce-scatter.9.cloned.1.call-done = f32[768,256]{1,0:T(8,128)} async-done(((f32[3072,256]{1,0:T(8,128)}), f32[768,256]{1,0:T(8,128)}) %reduce-scatter.9.cloned.1.call-update) | async-done | bytes 786448 | tf_op jit(solution)/shard_map/reduce_scatter | solution.py:24
  124.0 1.8 collective-permute-start
  125.8 73.6 %psum.56 = f32[256]{0:T(256)S(1)} all-reduce(f32[256]{0:T(256)S(1)} %get-tuple-element.20), channel_id=1, replica_groups=mesh['col'=4,'row'=8] {'col','row'}, use_global_device_ids=true, to_apply=%region_2.0 | all-reduce | flops 256 | bytes 2048 | tf_op jit(solution)/shard_map/psum | solution.py:21
  199.4 0.9 fusion
  200.4 31.0 %all-gather.11.cloned.1.call-done = bf16[6144,256]{1,0:T(8,128)(2,1)} async-done(((bf16[768,256]{1,0:T(8,128)(2,1)}), bf16[6144,256]{1,0:T(8,128)(2,1)}) %all-gather.11.cloned.1.call-update) | async-done | bytes 3145744 | tf_op jit(solution)/shard_map/all_gather | solution.py:22
  231.4 19.0 %convolution_bitcast_fusion.6 = f32[3072,256]{1,0:T(8,128)} fusion(bf16[3072,6144]{1,0:T(8,128)(2,1)} %param.4, bf16[6144,256]{1,0:T(8,128)(2,1)} %all-gather.11.cloned.1.call-done), kind=kOutput, calls=%fused_computation.6 | convolution fusion | flops 9663676416 | bytes 44040192 | tf_op jit(solution)/shard_map/dot_general | solution.py:23
  250.5 60.6 %reduce-scatter.11.cloned.1.call-done = f32[768,256]{1,0:T(8,128)} async-done(((f32[3072,256]{1,0:T(8,128)}), f32[768,256]{1,0:T(8,128)}) %reduce-scatter.11.cloned.1.call-update) | async-done | bytes 786448 | tf_op jit(solution)/shard_map/reduce_scatter | solution.py:24
  311.1 1.8 collective-permute-start.1
  312.8 73.6 %psum.57 = f32[256]{0:T(256)S(1)} all-reduce(f32[256]{0:T(256)S(1)} %get-tuple-element.18), channel_id=1, replica_groups=mesh['col'=4,'row'=8] {'col','row'}, use_global_device_ids=true, to_apply=%region_5.0 | all-reduce | flops 256 | bytes 2048 | tf_op jit(solution)/shard_map/psum | solution.py:21
  386.4 0.9 fusion.1
  387.4 31.0 %all-gather.13.cloned.1.call-done = bf16[6144,256]{1,0:T(8,128)(2,1)} async-done(((bf16[768,256]{1,0:T(8,128)(2,1)}), bf16[6144,256]{1,0:T(8,128)(2,1)}) %all-gather.13.cloned.1.call-update) | async-done | bytes 3145744 | tf_op jit(solution)/shard_map/all_gather | solution.py:22
  418.4 19.0 %convolution_bitcast_fusion.5 = f32[3072,256]{1,0:T(8,128)} fusion(bf16[3072,6144]{1,0:T(8,128)(2,1)} %param.4, bf16[6144,256]{1,0:T(8,128)(2,1)} %all-gather.13.cloned.1.call-done), kind=kOutput, calls=%fused_computation.5 | convolution fusion | flops 9663676416 | bytes 44040192 | tf_op jit(solution)/shard_map/dot_general | solution.py:23
  437.5 60.6 %reduce-scatter.13.cloned.1.call-done = f32[768,256]{1,0:T(8,128)} async-done(((f32[3072,256]{1,0:T(8,128)}), f32[768,256]{1,0:T(8,128)}) %reduce-scatter.13.cloned.1.call-update) | async-done | bytes 786448 | tf_op jit(solution)/shard_map/reduce_scatter | solution.py:24
  498.1 1.8 collective-permute-start.2
  499.9 73.6 %psum.58 = f32[256]{0:T(256)S(1)} all-reduce(f32[256]{0:T(256)S(1)} %get-tuple-element.16), channel_id=1, replica_groups=mesh['col'=4,'row'=8] {'col','row'}, use_global_device_ids=true, to_apply=%region_8.0 | all-reduce | flops 256 | bytes 2048 | tf_op jit(solution)/shard_map/psum | solution.py:21
  573.5 0.9 fusion.2
  574.4 31.0 %all-gather.15.cloned.1.call-done = bf16[6144,256]{1,0:T(8,128)(2,1)} async-done(((bf16[768,256]{1,0:T(8,128)(2,1)}), bf16[6144,256]{1,0:T(8,128)(2,1)}) %all-gather.15.cloned.1.call-update) | async-done | bytes 3145744 | tf_op jit(solution)/shard_map/all_gather | solution.py:22
  605.4 19.0 %convolution_bitcast_fusion.4 = f32[3072,256]{1,0:T(8,128)} fusion(bf16[3072,6144]{1,0:T(8,128)(2,1)} %param.4, bf16[6144,256]{1,0:T(8,128)(2,1)} %all-gather.15.cloned.1.call-done), kind=kOutput, calls=%fused_computation.4 | convolution fusion | flops 9663676416 | bytes 44040192 | tf_op jit(solution)/shard_map/dot_general | solution.py:23
  624.5 60.6 %reduce-scatter.15.cloned.1.call-done = f32[768,256]{1,0:T(8,128)} async-done(((f32[3072,256]{1,0:T(8,128)}), f32[768,256]{1,0:T(8,128)}) %reduce-scatter.15.cloned.1.call-update) | async-done | bytes 786448 | tf_op jit(solution)/shard_map/reduce_scatter | solution.py:24
  685.1 1.9 collective-permute-start.3
  687.0 73.4 %psum.59 = f32[256]{0:T(256)S(1)} all-reduce(f32[256]{0:T(256)S(1)} %get-tuple-element.14), channel_id=1, replica_groups=mesh['col'=4,'row'=8] {'col','row'}, use_global_device_ids=true, to_apply=%region_11.0 | all-reduce | flops 256 | bytes 2048 | tf_op jit(solution)/shard_map/psum | solution.py:21
  760.5 0.9 fusion.3
  761.5 31.0 %all-gather.17.cloned.1.call-done = bf16[6144,256]{1,0:T(8,128)(2,1)} async-done(((bf16[768,256]{1,0:T(8,128)(2,1)}), bf16[6144,256]{1,0:T(8,128)(2,1)}) %all-gather.17.cloned.1.call-update) | async-done | bytes 3145744 | tf_op jit(solution)/shard_map/all_gather | solution.py:22
  792.4 19.0 %convolution_bitcast_fusion.3 = f32[3072,256]{1,0:T(8,128)} fusion(bf16[3072,6144]{1,0:T(8,128)(2,1)} %param.4, bf16[6144,256]{1,0:T(8,128)(2,1)} %all-gather.17.cloned.1.call-done), kind=kOutput, calls=%fused_computation.3 | convolution fusion | flops 9663676416 | bytes 44040192 | tf_op jit(solution)/shard_map/dot_general | solution.py:23
  811.6 60.6 %reduce-scatter.17.cloned.1.call-done = f32[768,256]{1,0:T(8,128)} async-done(((f32[3072,256]{1,0:T(8,128)}), f32[768,256]{1,0:T(8,128)}) %reduce-scatter.17.cloned.1.call-update) | async-done | bytes 786448 | tf_op jit(solution)/shard_map/reduce_scatter | solution.py:24
  872.1 1.8 collective-permute-start.4
  873.9 73.6 %psum.60 = f32[256]{0:T(256)S(1)} all-reduce(f32[256]{0:T(256)S(1)} %get-tuple-element.12), channel_id=1, replica_groups=mesh['col'=4,'row'=8] {'col','row'}, use_global_device_ids=true, to_apply=%region_14.0 | all-reduce | flops 256 | bytes 2048 | tf_op jit(solution)/shard_map/psum | solution.py:21
  947.5 0.9 fusion.4
  948.5 31.0 %all-gather.19.cloned.1.call-done = bf16[6144,256]{1,0:T(8,128)(2,1)} async-done(((bf16[768,256]{1,0:T(8,128)(2,1)}), bf16[6144,256]{1,0:T(8,128)(2,1)}) %all-gather.19.cloned.1.call-update) | async-done | bytes 3145744 | tf_op jit(solution)/shard_map/all_gather | solution.py:22
  979.5 19.0 %convolution_bitcast_fusion.2 = f32[3072,256]{1,0:T(8,128)} fusion(bf16[3072,6144]{1,0:T(8,128)(2,1)} %param.4, bf16[6144,256]{1,0:T(8,128)(2,1)} %all-gather.19.cloned.1.call-done), kind=kOutput, calls=%fused_computation.2 | convolution fusion | flops 9663676416 | bytes 44040192 | tf_op jit(solution)/shard_map/dot_general | solution.py:23
  998.6 60.6 %reduce-scatter.19.cloned.1.call-done = f32[768,256]{1,0:T(8,128)} async-done(((f32[3072,256]{1,0:T(8,128)}), f32[768,256]{1,0:T(8,128)}) %reduce-scatter.19.cloned.1.call-update) | async-done | bytes 786448 | tf_op jit(solution)/shard_map/reduce_scatter | solution.py:24
  1059.1 2.0 collective-permute-start.5
  1061.1 73.6 %psum.61 = f32[256]{0:T(256)S(1)} all-reduce(f32[256]{0:T(256)S(1)} %get-tuple-element.10), channel_id=1, replica_groups=mesh['col'=4,'row'=8] {'col','row'}, use_global_device_ids=true, to_apply=%region_17.0 | all-reduce | flops 256 | bytes 2048 | tf_op jit(solution)/shard_map/psum | solution.py:21
  1135.7 31.0 %all-gather.21.cloned.1.call-done = bf16[6144,256]{1,0:T(8,128)(2,1)} async-done(((bf16[768,256]{1,0:T(8,128)(2,1)}), bf16[6144,256]{1,0:T(8,128)(2,1)}) %all-gather.21.cloned.1.call-update) | async-done | bytes 3145744 | tf_op jit(solution)/shard_map/all_gather | solution.py:22
  1166.7 19.0 %convolution_bitcast_fusion.1 = f32[3072,256]{1,0:T(8,128)} fusion(bf16[3072,6144]{1,0:T(8,128)(2,1)} %param.4, bf16[6144,256]{1,0:T(8,128)(2,1)} %all-gather.21.cloned.1.call-done), kind=kOutput, calls=%fused_computation.1 | convolution fusion | flops 9663676416 | bytes 44040192 | tf_op jit(solution)/shard_map/dot_general | solution.py:23
  1185.8 60.6 %reduce-scatter.21.cloned.1.call-done = f32[768,256]{1,0:T(8,128)} async-done(((f32[3072,256]{1,0:T(8,128)}), f32[768,256]{1,0:T(8,128)}) %reduce-scatter.21.cloned.1.call-update) | async-done | bytes 786448 | tf_op jit(solution)/shard_map/reduce_scatter | solution.py:24
  1246.3 1.8 collective-permute-start.6
  1248.1 73.6 %psum.62 = f32[256]{0:T(256)S(1)} all-reduce(f32[256]{0:T(256)S(1)} %get-tuple-element.8), channel_id=1, replica_groups=mesh['col'=4,'row'=8] {'col','row'}, use_global_device_ids=true, to_apply=%region_20.0 | all-reduce | flops 256 | bytes 2048 | tf_op jit(solution)/shard_map/psum | solution.py:21
  1321.7 0.9 multiply_reduce_fusion
  1322.9 30.7 %all-gather.23.cloned.1.call-done = bf16[6144,256]{1,0:T(8,128)(2,1)} async-done(((bf16[768,256]{1,0:T(8,128)(2,1)}), bf16[6144,256]{1,0:T(8,128)(2,1)}) %all-gather.23.cloned.1.call-update) | async-done | bytes 3145744 | tf_op jit(solution)/shard_map/all_gather | solution.py:22
  1353.7 19.0 %convolution_bitcast_fusion = f32[3072,256]{1,0:T(8,128)} fusion(bf16[3072,6144]{1,0:T(8,128)(2,1)} %param.4, bf16[6144,256]{1,0:T(8,128)(2,1)} %all-gather.23.cloned.1.call-done), kind=kOutput, calls=%fused_computation | convolution fusion | flops 9663676416 | bytes 44040192 | tf_op jit(solution)/shard_map/dot_general | solution.py:23
  1372.7 60.6 %reduce-scatter.23.cloned.1.call-done = f32[768,256]{1,0:T(8,128)} async-done(((f32[3072,256]{1,0:T(8,128)}), f32[768,256]{1,0:T(8,128)}) %reduce-scatter.23.cloned.1.call-update) | async-done | bytes 786448 | tf_op jit(solution)/shard_map/reduce_scatter | solution.py:24
  1433.3 1.8 collective-permute-start.7
  1435.1 73.6 %psum.63 = f32[256]{0:T(256)S(1)} all-reduce(f32[256]{0:T(256)S(1)} %get-tuple-element.5), channel_id=1, replica_groups=mesh['col'=4,'row'=8] {'col','row'}, use_global_device_ids=true, to_apply=%region_23.0 | all-reduce | flops 256 | bytes 2048 | tf_op jit(solution)/shard_map/psum | solution.py:21
  1508.7 1.1 multiply_add_fusion
  (52 shorter events, 2.8 us)
Async XLA Ops:
  6.5 37.8 %all-gather.9.cloned.1.call-start = ((), (), s32[]{:S(2)}) async-start(), calls=%async_computation.8 | async-start | bytes 3538944 | tf_op jit(solution)/shard_map/all_gather | solution.py:22
  9.6 114.5 %reduce-scatter.9.cloned.1.call-start = ((), (), s32[]{:S(2)}) async-start(), calls=%async_computation.9 | async-start | bytes 3932160 | tf_op jit(solution)/shard_map/reduce_scatter | solution.py:24
  63.4 136.0 %copy-start = (f32[768,256]{1,0:T(8,128)S(1)}, f32[768,256]{1,0:T(8,128)}, u32[]{:S(2)}) copy-start(f32[768,256]{1,0:T(8,128)} %param.6) | copy-start | bytes 2359300
  63.4 168.0 %all-gather.11.cloned.1.call-start = ((), (), s32[]{:S(2)}) async-start(), calls=%async_computation.10 | async-start | bytes 3538944 | tf_op jit(solution)/shard_map/all_gather | solution.py:22
  124.0 75.4 %collective-permute-start = (f32[768,256]{1,0:T(8,128)}, f32[768,256]{1,0:T(8,128)S(1)}, u32[]{:S(2)}, u32[]{:S(2)}) collective-permute-start(f32[768,256]{1,0:T(8,128)} %reduce-scatter.9.cloned.1.call-done), channel_id=1, source_target_pairs={{0,0},{8,1},{16,2},{24,3},{1,4},{9,5},{17,6},{25,7},{2,8},{10,9},{... | collective-permute-start | bytes 2359304 | tf_op jit(solution)/shard_map/ppermute | solution.py:25
  200.4 110.7 %reduce-scatter.11.cloned.1.call-start = ((), (), s32[]{:S(2)}) async-start(), calls=%async_computation.11 | async-start | bytes 3932160 | tf_op jit(solution)/shard_map/reduce_scatter | solution.py:24
  250.5 168.0 %all-gather.13.cloned.1.call-start = ((), (), s32[]{:S(2)}) async-start(), calls=%async_computation.12 | async-start | bytes 3538944 | tf_op jit(solution)/shard_map/all_gather | solution.py:22
  311.1 75.4 %collective-permute-start.1 = (f32[768,256]{1,0:T(8,128)}, f32[768,256]{1,0:T(8,128)S(1)}, u32[]{:S(2)}, u32[]{:S(2)}) collective-permute-start(f32[768,256]{1,0:T(8,128)} %reduce-scatter.11.cloned.1.call-done), channel_id=1, source_target_pairs={{0,0},{8,1},{16,2},{24,3},{1,4},{9,5},{17,6},{25,7},{2,8},{10,9},{... | collective-permute-start | bytes 2359304 | tf_op jit(solution)/shard_map/ppermute | solution.py:25
  387.4 110.7 %reduce-scatter.13.cloned.1.call-start = ((), (), s32[]{:S(2)}) async-start(), calls=%async_computation.13 | async-start | bytes 3932160 | tf_op jit(solution)/shard_map/reduce_scatter | solution.py:24
  437.5 168.0 %all-gather.15.cloned.1.call-start = ((), (), s32[]{:S(2)}) async-start(), calls=%async_computation.14 | async-start | bytes 3538944 | tf_op jit(solution)/shard_map/all_gather | solution.py:22
  498.1 75.4 %collective-permute-start.2 = (f32[768,256]{1,0:T(8,128)}, f32[768,256]{1,0:T(8,128)S(1)}, u32[]{:S(2)}, u32[]{:S(2)}) collective-permute-start(f32[768,256]{1,0:T(8,128)} %reduce-scatter.13.cloned.1.call-done), channel_id=1, source_target_pairs={{0,0},{8,1},{16,2},{24,3},{1,4},{9,5},{17,6},{25,7},{2,8},{10,9},{... | collective-permute-start | bytes 2359304 | tf_op jit(solution)/shard_map/ppermute | solution.py:25
  574.4 110.7 %reduce-scatter.15.cloned.1.call-start = ((), (), s32[]{:S(2)}) async-start(), calls=%async_computation.15 | async-start | bytes 3932160 | tf_op jit(solution)/shard_map/reduce_scatter | solution.py:24
  624.5 168.0 %all-gather.17.cloned.1.call-start = ((), (), s32[]{:S(2)}) async-start(), calls=%async_computation.16 | async-start | bytes 3538944 | tf_op jit(solution)/shard_map/all_gather | solution.py:22
  685.1 75.4 %collective-permute-start.3 = (f32[768,256]{1,0:T(8,128)}, f32[768,256]{1,0:T(8,128)S(1)}, u32[]{:S(2)}, u32[]{:S(2)}) collective-permute-start(f32[768,256]{1,0:T(8,128)} %reduce-scatter.15.cloned.1.call-done), channel_id=1, source_target_pairs={{0,0},{8,1},{16,2},{24,3},{1,4},{9,5},{17,6},{25,7},{2,8},{10,9},{... | collective-permute-start | bytes 2359304 | tf_op jit(solution)/shard_map/ppermute | solution.py:25
  761.4 110.7 %reduce-scatter.17.cloned.1.call-start = ((), (), s32[]{:S(2)}) async-start(), calls=%async_computation.17 | async-start | bytes 3932160 | tf_op jit(solution)/shard_map/reduce_scatter | solution.py:24
  811.5 168.0 %all-gather.19.cloned.1.call-start = ((), (), s32[]{:S(2)}) async-start(), calls=%async_computation.18 | async-start | bytes 3538944 | tf_op jit(solution)/shard_map/all_gather | solution.py:22
  872.1 75.4 %collective-permute-start.4 = (f32[768,256]{1,0:T(8,128)}, f32[768,256]{1,0:T(8,128)S(1)}, u32[]{:S(2)}, u32[]{:S(2)}) collective-permute-start(f32[768,256]{1,0:T(8,128)} %reduce-scatter.17.cloned.1.call-done), channel_id=1, source_target_pairs={{0,0},{8,1},{16,2},{24,3},{1,4},{9,5},{17,6},{25,7},{2,8},{10,9},{... | collective-permute-start | bytes 2359304 | tf_op jit(solution)/shard_map/ppermute | solution.py:25
  948.4 110.7 %reduce-scatter.19.cloned.1.call-start = ((), (), s32[]{:S(2)}) async-start(), calls=%async_computation.19 | async-start | bytes 3932160 | tf_op jit(solution)/shard_map/reduce_scatter | solution.py:24
  998.5 168.1 %all-gather.21.cloned.1.call-start = ((), (), s32[]{:S(2)}) async-start(), calls=%async_computation.20 | async-start | bytes 3538944 | tf_op jit(solution)/shard_map/all_gather | solution.py:22
  1059.1 75.6 %collective-permute-start.5 = (f32[768,256]{1,0:T(8,128)}, f32[768,256]{1,0:T(8,128)S(1)}, u32[]{:S(2)}, u32[]{:S(2)}) collective-permute-start(f32[768,256]{1,0:T(8,128)} %reduce-scatter.19.cloned.1.call-done), channel_id=1, source_target_pairs={{0,0},{8,1},{16,2},{24,3},{1,4},{9,5},{17,6},{25,7},{2,8},{10,9},{... | collective-permute-start | bytes 2359304 | tf_op jit(solution)/shard_map/ppermute | solution.py:25
  1135.6 110.7 %reduce-scatter.21.cloned.1.call-start = ((), (), s32[]{:S(2)}) async-start(), calls=%async_computation.21 | async-start | bytes 3932160 | tf_op jit(solution)/shard_map/reduce_scatter | solution.py:24
  1185.7 168.0 %all-gather.23.cloned.1.call-start = ((), (), s32[]{:S(2)}) async-start(), calls=%async_computation.22 | async-start | bytes 3538944 | tf_op jit(solution)/shard_map/all_gather | solution.py:22
  1246.3 75.4 %collective-permute-start.6 = (f32[768,256]{1,0:T(8,128)}, f32[768,256]{1,0:T(8,128)S(1)}, u32[]{:S(2)}, u32[]{:S(2)}) collective-permute-start(f32[768,256]{1,0:T(8,128)} %reduce-scatter.21.cloned.1.call-done), channel_id=1, source_target_pairs={{0,0},{8,1},{16,2},{24,3},{1,4},{9,5},{17,6},{25,7},{2,8},{10,9},{... | collective-permute-start | bytes 2359304 | tf_op jit(solution)/shard_map/ppermute | solution.py:25
  1322.6 110.7 %reduce-scatter.23.cloned.1.call-start = ((), (), s32[]{:S(2)}) async-start(), calls=%async_computation.23 | async-start | bytes 3932160 | tf_op jit(solution)/shard_map/reduce_scatter | solution.py:24
  1433.3 75.4 %collective-permute-start.7 = (f32[768,256]{1,0:T(8,128)}, f32[768,256]{1,0:T(8,128)S(1)}, u32[]{:S(2)}, u32[]{:S(2)}) collective-permute-start(f32[768,256]{1,0:T(8,128)} %reduce-scatter.23.cloned.1.call-done), channel_id=1, source_target_pairs={{0,0},{8,1},{16,2},{24,3},{1,4},{9,5},{17,6},{25,7},{2,8},{10,9},{... | collective-permute-start | bytes 2359304 | tf_op jit(solution)/shard_map/ppermute | solution.py:25
Sparse Core Ops, SparseCore 0:
  9.7 34.6 all-gather.8
  63.6 60.4 reduce-scatter.8
  200.5 30.8 all-gather.10
  250.6 60.4 reduce-scatter.10
  387.5 30.8 all-gather.12
  437.6 60.4 reduce-scatter.12
  574.5 30.8 all-gather.14
  624.6 60.4 reduce-scatter.14
  761.5 30.8 all-gather.16
  811.6 60.4 reduce-scatter.16
  948.5 30.8 all-gather.18
  998.6 60.4 reduce-scatter.18
  1135.7 30.8 all-gather.20
  1185.8 60.4 reduce-scatter.20
  1322.8 30.8 all-gather.22
  1372.9 60.4 reduce-scatter.22
where the time goes:
time: 1530 us; the launch traced here: 1520 us
  waiting for transfers between devices  736 us (48%)
  blocking collectives  589 us (38%)
  matrix products  152 us (10%)
  starting transfers between devices  15.5 us (1%)
    psum x8, blocking collectives, local_sweeps(): lax.psum(jnp.sum(dang_col * x_cur, axis=0), ('col', 'row')) / vertex_count  589 us
    reduce_scatter x8, waiting for transfers between devices, local_sweeps(): folded = lax.psum_scatter(part_prod, 'col', scatter_dimension=0, tiled=True)  484 us
    all_gather x8, waiting for transfers between devices, local_sweeps(): lax.all_gather(x_cur.astype(jnp.bfloat16), 'row', axis=0, tiled=True)  251 us
    dot_general x8, matrix products, local_sweeps(): part_prod = jnp.dot(mat_tile, x_src, preferred_element_type=jnp.float32)  152 us
  transfers between devices with their start and end apart: 24, of which 16 were waited for; matrix products, arithmetic and copies ran while one was open for 0% of the time, Pallas kernels for 0%

commit v1 on v0

v1 whole, which is shorter than its diff:
```python
import functools

import jax
import jax.numpy as jnp
from jax import lax
from jax.experimental import pallas as pl
from jax.experimental.pallas import tpu as pltpu
from jax.sharding import PartitionSpec as P

SWEEPS = 8
DAMPING = 0.85
MESH = pl.DeviceIdType.MESH

CHUNKS = 8
PERIOD = 8
HOP = 2
GATHER = 2
FORWARD = 3
READY = 3
RING = 4
PASSES = 2 * SWEEPS


def kernel(block_rows, lanes, a_hbm, x_ref, v_ref, d_ref, out_ref,
           a_v, xbuf, rbuf, sums, xs, vbuf, dbuf, sacc, sstage, sbuf, coef,
           a_sem, r_send, r_recv, z_send, z_recv, g_send, g_recv, f_send, f_recv,
           s_send, s_recv, v_send, v_recv, d_send, d_recv, x0_send, x0_recv, x1_send, x1_recv, o_recv):
    z = lax.axis_index('col')
    row = lax.axis_index('row')
    k = row % 2
    x = (row // 2) % 2
    y = row // 4
    c = row // 2
    half = block_rows // 2
    ch = half // CHUNKS
    sub = ch // 4
    piece = block_rows // 4
    vertices = block_rows * 8
    inplane = (y * 4 + (1 - x) * 2 + k, (1 - y) * 4 + x * 2 + k, (1 - y) * 4 + (1 - x) * 2 + k)
    partner = c * 2 + (1 - k)

    def remote(src, dst, send, recv, dev):
        return pltpu.make_async_remote_copy(src_ref=src, dst_ref=dst, send_sem=send, recv_sem=recv,
                                            device_id=dev, device_id_type=MESH)

    def a_copy(dirn, q):
        rows = pl.ds(dirn * half + q * ch, ch)
        return pltpu.make_async_copy(a_hbm.at[rows], a_v.at[rows], a_sem.at[dirn, q])

    def start_a(q, carry):
        for dirn in range(2):
            a_copy(dirn, q).start()
        return carry
    lax.fori_loop(0, CHUNKS, start_a, 0)

    barrier = pltpu.get_barrier_semaphore()
    me = z * 8 + row

    def greet(step, carry):
        other = (me + step) % 32
        pl.semaphore_signal(barrier, inc=1, device_id=(other // 8, other % 8), device_id_type=MESH)
        return carry
    lax.fori_loop(1, 32, greet, 0)
    pl.semaphore_wait(barrier, 31)

    def x_rows(h, par, start, size):
        return xbuf.at[h, par, pl.ds(start, size)]

    def x0_copy(h, m):
        dev = inplane[m] if m < 3 else partner
        mine = x_rows(h, 0, row * piece, piece)
        return remote(mine, mine, x0_send.at[h, m], x0_recv.at[h, m], (z, dev))

    def x1_copy(h, m):
        theirs = x_rows(h, 0, inplane[m] * piece, piece)
        return remote(theirs, theirs, x1_send.at[h, m], x1_recv.at[h, m], (z, partner))

    for h in range(2):
        xbuf[h, 0, pl.ds(row * piece, piece), :] = x_ref[:, h * lanes:(h + 1) * lanes].astype(jnp.bfloat16)
        for m in range(4):
            x0_copy(h, m).start()

    def s_copy(h, holder):
        dev = (holder // 2, (holder // 2) * 2 + holder % 2)
        return remote(sstage.at[h], sbuf.at[h, me], s_send.at[h, holder], s_recv.at[h, me], dev)

    holds_v = c == z

    def s_start(h):
        for holder in range(8):
            mine = (holder // 2 == z) & ((holder // 2) * 2 + holder % 2 == row)

            @pl.when(mine)
            def _():
                sbuf[h, me] = sstage[h]

            @pl.when(jnp.logical_not(mine))
            def _():
                s_copy(h, holder).start()

    def s_wait_send(h):
        for holder in range(8):
            @pl.when(jnp.logical_not((holder // 2 == z) & ((holder // 2) * 2 + holder % 2 == row)))
            def _():
                s_copy(h, holder).wait_send()

    for h in range(2):
        terms = d_ref[...].astype(jnp.float32) * x_ref[:, h * lanes:(h + 1) * lanes]
        sstage[h] = jnp.sum(terms.reshape(piece // 8, 8, lanes), axis=0)
        s_start(h)

    v_dev = z * 2 + row // 4
    v_self = v_dev == row

    def v_copy(h):
        return remote(v_ref.at[:, pl.ds(h * lanes, lanes)], vbuf.at[h, pl.ds((row % 4) * piece, piece)],
                      v_send.at[h], v_recv.at[h, row % 4], (z, v_dev))

    @pl.when(v_self)
    def _():
        for h in range(2):
            vbuf[h, pl.ds((row % 4) * piece, piece), :] = v_ref[:, h * lanes:(h + 1) * lanes]

    d_plane = ((row % 4) // 2) * 3
    d_self = v_self & (d_plane == z)
    d_copy = remote(d_ref, dbuf.at[pl.ds((row % 2) * piece, piece)], d_send, d_recv.at[row % 2], (d_plane, v_dev))

    @pl.when(d_self)
    def _():
        dbuf[pl.ds((row % 2) * piece, piece), :] = d_ref[...]

    @pl.when(jnp.logical_not(v_self))
    def _():
        for h in range(2):
            v_copy(h).start()

    @pl.when(jnp.logical_not(d_self))
    def _():
        d_copy.start()

    for h in range(2):
        for m in range(3):
            x0_copy(h, m).wait_recv()
            x1_copy(h, m).start()
    for h in range(2):
        x0_copy(h, 3).wait_recv()
        for m in range(3):
            x1_copy(h, m).wait_recv()
        for m in range(4):
            x0_copy(h, m).wait_send()
        for m in range(3):
            x1_copy(h, m).wait_send()

    def index(step):
        n = step // PERIOD
        q = step % PERIOD
        valid = (step >= 0) & (n < PASSES) & (q < CHUNKS)
        return valid, n, q, n % 2, (n // 2) % 2

    def owner_is_reader(dirn):
        return (z == c) & (z == 3 * dirn)

    def slot(t, carry):
        def gather_copy(h, par, dirn, q, ring, m):
            rows = x_rows(h, 1 - par, k * block_rows + dirn * half + q * ch + c * sub, sub)
            return remote(rows, rows, g_send.at[ring, dirn, m], g_recv.at[h, dirn, q, m], (z, inplane[m]))

        def forward_copy(h, par, dirn, q, ring):
            rows = x_rows(h, 1 - par, k * block_rows + dirn * half + q * ch, ch)
            return remote(rows, rows, f_send.at[ring, dirn], f_recv.at[h, dirn, q], (z, partner))

        def forward(dirn):
            step = t - 3 * HOP - FORWARD
            old, n, q, h, par = index(step - RING)

            @pl.when(old & (n < PASSES - 2))
            def _():
                forward_copy(h, par, dirn, q, (step - RING) % RING).wait_send()
            valid, n, q, h, par = index(step)

            @pl.when(valid & (n < PASSES - 2))
            def _():
                for m in range(3):
                    gather_copy(h, par, dirn, q, step % RING, m).wait_recv()
                forward_copy(h, par, dirn, q, step % RING).start()

        def ready(dirn):
            step = t - 3 * HOP - READY
            valid, n, q, h, par = index(step)

            @pl.when(valid & (n < PASSES - 2))
            def _():
                forward_copy(h, par, dirn, q, step % RING).wait_recv()

        def gather(dirn):
            step = t - 3 * HOP - GATHER
            old, n, q, h, par = index(step - RING)

            @pl.when(old & (n < PASSES - 2))
            def _():
                for m in range(3):
                    gather_copy(h, par, dirn, q, (step - RING) % RING, m).wait_send()
            valid, n, q, h, par = index(step)

            @pl.when(valid & (n < PASSES - 2))
            def _():
                @pl.when(jnp.logical_not(owner_is_reader(dirn)))
                def _():
                    rows = x_rows(h, 1 - par, k * block_rows + dirn * half + q * ch + c * sub, sub)
                    remote(rows, rows, z_send.at[0, 0], z_recv.at[h, dirn, q], (z, row)).wait_recv()
                for m in range(3):
                    gather_copy(h, par, dirn, q, step % RING, m).start()

        def dangling_term():
            near = jnp.minimum(z, 3 - z)
            step = t - HOP * near
            valid, n, q, h, par = index(step)

            @pl.when(holds_v & valid & (q == 0))
            def _():
                def wait_one(src, carry):
                    sends = ((n < 2) | (src // 8 == 0) | (src // 8 == 3)) & (src != me)

                    @pl.when(sends)
                    def _():
                        remote(sstage.at[h], sbuf.at[h, src], s_send.at[h, 0], s_recv.at[h, src], (z, row)).wait_recv()
                    return carry
                lax.fori_loop(0, 32, wait_one, 0)

                @pl.when(n < 2)
                def _():
                    for piece_idx in range(4):
                        @pl.when(4 * k + piece_idx != row)
                        def _():
                            rows = vbuf.at[h, pl.ds(piece_idx * piece, piece)]
                            remote(rows, rows, v_send.at[0], v_recv.at[h, piece_idx], (z, row)).wait_recv()
                ends = jnp.sum(sbuf[h, 0:8], axis=0) + jnp.sum(sbuf[h, 24:32], axis=0)
                coef[h] = ends

                @pl.when(n < 2)
                def _():
                    coef[h] += jnp.sum(sbuf[h, 8:24], axis=0)
                mass = jnp.sum(coef[h], axis=0, keepdims=True) / vertices
                coef[h] = jnp.broadcast_to(DAMPING * mass + (1.0 - DAMPING), (8, lanes))

        def reduce(dirn):
            pos = z if dirn == 1 else 3 - z
            after = z + 1 if dirn == 1 else z - 1
            owner = pos == 3

            def sum_copy(h, q, ring):
                return remote(sums.at[dirn, ring], rbuf.at[dirn, h, q], r_send.at[dirn, ring], r_recv.at[dirn, h, q],
                              (after, row))

            def out_place(h, q):
                rows = pl.ds((q % 4) * ch, ch)
                return out_ref.at[rows, pl.ds(pl.multiple_of(h * lanes, lanes), lanes)]

            def out_row(q):
                return 4 * k + 2 * dirn + q // 4

            def out_here(q):
                return (z == c) & (out_row(q) == row)

            def out_copy(h, q, ring):
                return remote(sums.at[dirn, ring], out_place(h, q), r_send.at[dirn, ring], o_recv.at[h, q % 4],
                              (c, out_row(q)))

            def share_copy(h, par, q, ring, cc):
                rows = x_rows(h, 1 - par, k * block_rows + dirn * half + q * ch + cc * sub, sub)
                return remote(xs.at[ring, pl.ds(cc * sub, sub)], rows, z_send.at[ring, cc], z_recv.at[h, dirn, q],
                              (c, 2 * cc + k))

            step = t - HOP * pos
            old, n, q, h, par = index(step - RING)
            ring = (step - RING) % RING

            @pl.when(old & jnp.logical_not(owner))
            def _():
                sum_copy(h, q, ring).wait_send()

            @pl.when(old & owner & (n < PASSES - 2))
            def _():
                for cc in range(4):
                    @pl.when(jnp.logical_not((z == c) & (cc == c)))
                    def _():
                        share_copy(h, par, q, ring, cc).wait_send()

                @pl.when(q == CHUNKS - 1)
                def _():
                    s_wait_send(h)

            @pl.when(old & owner & (n >= PASSES - 2) & jnp.logical_not(out_here(q)))
            def _():
                out_copy(h, q, ring).wait_send()

            valid, n, q, h, par = index(step)
            ring = step % RING

            @pl.when(valid)
            def _():
                start = dirn * half + q * ch
                rows = pl.ds(start, ch)

                @pl.when(n == 0)
                def _():
                    a_copy(dirn, q).wait()
                prod = jnp.dot(a_v[rows, :], xbuf[h, par], preferred_element_type=jnp.float32)
                sums[dirn, ring] = prod * DAMPING

                @pl.when(holds_v)
                def _():
                    sums[dirn, ring] += coef[h, 0:1, :] * vbuf[h, rows, :]

                @pl.when(pos > 0)
                def _():
                    sum_copy(h, q, ring).wait_recv()
                    sums[dirn, ring] += rbuf[dirn, h, q]

                @pl.when(jnp.logical_not(owner))
                def _():
                    sum_copy(h, q, ring).start()

                @pl.when(owner & (n < PASSES - 2))
                def _():
                    @pl.when((n == 0) & (q == 0))
                    def _():
                        for part in range(2):
                            @pl.when(jnp.logical_not((z == c) & (4 * k + 2 * dirn + part == row)))
                            def _():
                                place = dbuf.at[pl.ds(part * piece, piece)]
                                remote(d_ref, place, d_send, d_recv.at[part], (z, row)).wait_recv()
                    total = sums[dirn, ring]
                    low = total.astype(jnp.bfloat16)
                    xs[ring] = low
                    terms = dbuf[pl.ds(q * ch, ch), :].astype(jnp.float32) * total
                    mass = jnp.sum(terms.reshape(ch // 8, 8, lanes), axis=0)
                    for cc in range(4):
                        here = (z == c) & (cc == c)

                        @pl.when(here)
                        def _():
                            place = pl.ds(k * block_rows + start + cc * sub, sub)
                            xbuf[h, 1 - par, place, :] = low[cc * sub:(cc + 1) * sub]

                        @pl.when(jnp.logical_not(here))
                        def _():
                            share_copy(h, par, q, ring, cc).start()

                    @pl.when(q == 0)
                    def _():
                        sacc[...] = mass

                    @pl.when(q > 0)
                    def _():
                        sacc[...] += mass

                    @pl.when(q == CHUNKS - 1)
                    def _():
                        sstage[h] = sacc[...]
                        s_start(h)

                @pl.when(owner & (n >= PASSES - 2))
                def _():
                    @pl.when(out_here(q))
                    def _():
                        out_ref[pl.ds((q % 4) * ch, ch), pl.ds(pl.multiple_of(h * lanes, lanes), lanes)] = sums[dirn, ring]

                    @pl.when(jnp.logical_not(out_here(q)))
                    def _():
                        out_copy(h, q, ring).start()

        @pl.when(t == 1)
        def _():
            for h in range(2):
                s_wait_send(h)

            @pl.when(jnp.logical_not(v_self))
            def _():
                for h in range(2):
                    v_copy(h).wait_send()

            @pl.when(jnp.logical_not(d_self))
            def _():
                d_copy.wait_send()

        for dirn in range(2):
            forward(dirn)
        for dirn in range(2):
            ready(dirn)
        dangling_term()
        reduce(1)
        for dirn in range(2):
            gather(dirn)
        reduce(0)
        return carry

    lax.fori_loop(0, PASSES * PERIOD + 3 * HOP + FORWARD + RING, slot, 0)

    made_here = (z == 3 * ((row % 4) // 2)) & (row == 2 * z + row // 4)

    @pl.when(jnp.logical_not(made_here))
    def _():
        for h in range(2):
            for q in range(4):
                place = out_ref.at[pl.ds(q * ch, ch), pl.ds(h * lanes, lanes)]
                remote(place, place, d_send, o_recv.at[h, q], (z, row)).wait_recv()


def solution(mesh):
    def local_sweeps(mat_tile, x_piece, tele_piece, dang_piece):
        block_rows, src = mat_tile.shape
        piece, vecs = x_piece.shape
        lanes = vecs // 2
        ch = block_rows // 2 // CHUNKS
        dang = jnp.broadcast_to(dang_piece.astype(jnp.bfloat16)[:, None], (piece, lanes))
        dma = pltpu.SemaphoreType.DMA
        return pl.pallas_call(
            functools.partial(kernel, block_rows, lanes),
            name='sweeps',
            out_shape=jax.ShapeDtypeStruct((piece, vecs), jnp.float32),
            in_specs=[pl.BlockSpec(memory_space=pltpu.HBM)] + [pl.BlockSpec(memory_space=pltpu.VMEM)] * 3,
            out_specs=pl.BlockSpec(memory_space=pltpu.VMEM),
            scratch_shapes=[
                pltpu.VMEM((block_rows, src), jnp.bfloat16),
                pltpu.VMEM((2, 2, src, lanes), jnp.bfloat16),
                pltpu.VMEM((2, 2, CHUNKS, ch, lanes), jnp.float32),
                pltpu.VMEM((2, RING, ch, lanes), jnp.float32),
                pltpu.VMEM((RING, ch, lanes), jnp.bfloat16),
                pltpu.VMEM((2, block_rows, lanes), jnp.float32),
                pltpu.VMEM((block_rows // 2, lanes), jnp.bfloat16),
                pltpu.VMEM((8, lanes), jnp.float32),
                pltpu.VMEM((2, 8, lanes), jnp.float32),
                pltpu.VMEM((2, 32, 8, lanes), jnp.float32),
                pltpu.VMEM((2, 8, lanes), jnp.float32),
                dma((2, CHUNKS)),
                dma((2, RING)),
                dma((2, 2, CHUNKS)),
                dma((RING, 4)),
                dma((2, 2, CHUNKS)),
                dma((RING, 2, 3)),
                dma((2, 2, CHUNKS, 3)),
                dma((RING, 2)),
                dma((2, 2, CHUNKS)),
                dma((2, 8)),
                dma((2, 32)),
                dma((2,)),
                dma((2, 4)),
                dma,
                dma((2,)),
                dma((2, 4)),
                dma((2, 4)),
                dma((2, 3)),
                dma((2, 3)),
                dma((2, 4)),
            ],
            compiler_params=pltpu.CompilerParams(collective_id=0, has_side_effects=True,
                                                 vmem_limit_bytes=64 * 1024 * 1024 - 65536),
        )(mat_tile, x_piece, tele_piece, dang)

    vec_spec = P(('col', 'row'), None)
    return jax.shard_map(local_sweeps, mesh=mesh,
                         in_specs=(P('row', 'col'), vec_spec, vec_spec, P(('col', 'row'))),
                         out_specs=vec_spec, check_vma=False)
```

time: 1530 us -> 789 us (0.52)
  Pallas kernels: 0 us -> 785 us
  waiting for transfers between devices: 736 us -> 0 us
  blocking collectives: 589 us -> 0 us
  matrix products: 152 us -> 0 us
  starting transfers between devices: 15.5 us -> 0 us
    pallas_call x0 -> x1, Pallas kernels: none -> 785 us  [local_sweeps(): pl.pallas_call(functools.partial(kernel, block_rows, lanes), name='sweeps...]
    psum x8 -> x0, blocking collectives: 589 us -> none  [local_sweeps(): lax.psum(jnp.sum(dang_col * x_cur, axis=0), ('col', 'row')) / vertex_count]
    reduce_scatter x8 -> x0, waiting for transfers between devices: 484 us -> none  [local_sweeps(): folded = lax.psum_scatter(part_prod, 'col', scatter_dimension=0, tiled=True)]
    all_gather x8 -> x0, waiting for transfers between devices: 251 us -> none  [local_sweeps(): lax.all_gather(x_cur.astype(jnp.bfloat16), 'row', axis=0, tiled=True)]
    dot_general x8 -> x0, matrix products: 152 us -> none  [local_sweeps(): part_prod = jnp.dot(mat_tile, x_src, preferred_element_type=jnp.float32)]
  transfers between devices with their start and end apart: 24 -> 0, of which waited for: 16 -> 0; matrix products, arithmetic and copies ran while one was open for 0% -> 0% of each run, Pallas kernels for 0% -> 0%
where the time goes in v1:
time: 789 us
  Pallas kernels  785 us (99%)
    pallas_call x1, Pallas kernels, local_sweeps(): pl.pallas_call(functools.partial(kernel, block_rows, lanes), name='sweeps...  785 us

profile of v1, /device:TPU:0, one launch (start us, length us, event | category | flops | bytes accessed | tf_op | source)
XLA Modules:
  0.0 788.8 jit_solution(6136934742400762982)
XLA Ops:
  0.0 0.7 convert_element_type.3
  0.7 0.8 broadcast_in_dim.2.d_ref
  1.5 785.1 %sweeps.1 = f32[768,256]{1,0:T(8,128)} custom-call(bf16[3072,6144]{1,0:T(8,128)(2,1)} %a_hbm.1, f32[768,256]{1,0:T(8,128)} %x_ref.1, f32[768,256]{1,0:T(8,128)} %v_ref.1, bf16[768,128]{1,0:T(8,128)(2,1)} %broadcast_in_dim.2.d_ref), custom_call_target="tpu_custom_call" | custom-call | tf_op jit(solution)/shard_map/sweeps/pallas_call | solution.py:418
  786.7 2.1 copy.6

commit v2 on v1

--- a/solution.py
+++ b/solution.py
@@ -11,12 +11,12 @@
 DAMPING = 0.85
 MESH = pl.DeviceIdType.MESH
 
-CHUNKS = 8
-PERIOD = 8
+CHUNKS = 12
+PERIOD = 12
 HOP = 2
-GATHER = 2
-FORWARD = 3
-READY = 3
+GATHER = 4
+FORWARD = 6
+READY = 7
 RING = 4
 PASSES = 2 * SWEEPS
 
@@ -53,6 +53,11 @@
         return carry
     lax.fori_loop(0, CHUNKS, start_a, 0)
 
+    for h in range(2):
+        xbuf[h, 0, pl.ds(row * piece, piece), :] = x_ref[:, h * lanes:(h + 1) * lanes].astype(jnp.bfloat16)
+        terms = d_ref[...].astype(jnp.float32) * x_ref[:, h * lanes:(h + 1) * lanes]
+        sstage[h] = jnp.sum(terms.reshape(piece // 8, 8, lanes), axis=0)
+
     barrier = pltpu.get_barrier_semaphore()
     me = z * 8 + row
 
@@ -75,10 +80,6 @@
         theirs = x_rows(h, 0, inplane[m] * piece, piece)
         return remote(theirs, theirs, x1_send.at[h, m], x1_recv.at[h, m], (z, partner))
 
-    for h in range(2):
-        xbuf[h, 0, pl.ds(row * piece, piece), :] = x_ref[:, h * lanes:(h + 1) * lanes].astype(jnp.bfloat16)
-        for m in range(4):
-            x0_copy(h, m).start()
 
     def s_copy(h, holder):
         dev = (holder // 2, (holder // 2) * 2 + holder % 2)
@@ -104,10 +105,6 @@
             def _():
                 s_copy(h, holder).wait_send()
 
-    for h in range(2):
-        terms = d_ref[...].astype(jnp.float32) * x_ref[:, h * lanes:(h + 1) * lanes]
-        sstage[h] = jnp.sum(terms.reshape(piece // 8, 8, lanes), axis=0)
-        s_start(h)
 
     v_dev = z * 2 + row // 4
     v_self = v_dev == row
@@ -129,20 +126,40 @@
     def _():
         dbuf[pl.ds((row % 2) * piece, piece), :] = d_ref[...]
 
-    @pl.when(jnp.logical_not(v_self))
-    def _():
-        for h in range(2):
+    for h in range(2):
+        s_start(h)
+    def x0_start(h):
+        for m in range(4):
+            x0_copy(h, m).start()
+
+    def v_start(h):
+        @pl.when(jnp.logical_not(v_self))
+        def _():
             v_copy(h).start()
 
+    x0_start(0)
+
+    @pl.when(k == 0)
+    def _():
+        v_start(0)
+        x0_start(1)
+
+    @pl.when(k == 1)
+    def _():
+        x0_start(1)
+        v_start(0)
+    v_start(1)
+
     @pl.when(jnp.logical_not(d_self))
     def _():
         d_copy.start()
 
-    for h in range(2):
+    def x0_forward(h):
         for m in range(3):
             x0_copy(h, m).wait_recv()
             x1_copy(h, m).start()
-    for h in range(2):
+
+    def x0_finish(h):
         x0_copy(h, 3).wait_recv()
         for m in range(3):
             x1_copy(h, m).wait_recv()
@@ -151,6 +168,9 @@
         for m in range(3):
             x1_copy(h, m).wait_send()
 
+    x0_forward(0)
+    x0_finish(0)
+
     def index(step):
         n = step // PERIOD
         q = step % PERIOD
@@ -227,13 +247,6 @@
                     return carry
                 lax.fori_loop(0, 32, wait_one, 0)
 
-                @pl.when(n < 2)
-                def _():
-                    for piece_idx in range(4):
-                        @pl.when(4 * k + piece_idx != row)
-                        def _():
-                            rows = vbuf.at[h, pl.ds(piece_idx * piece, piece)]
-                            remote(rows, rows, v_send.at[0], v_recv.at[h, piece_idx], (z, row)).wait_recv()
                 ends = jnp.sum(sbuf[h, 0:8], axis=0) + jnp.sum(sbuf[h, 24:32], axis=0)
                 coef[h] = ends
 
@@ -253,17 +266,17 @@
                               (after, row))
 
             def out_place(h, q):
-                rows = pl.ds((q % 4) * ch, ch)
+                rows = pl.ds((q % (CHUNKS // 2)) * ch, ch)
                 return out_ref.at[rows, pl.ds(pl.multiple_of(h * lanes, lanes), lanes)]
 
             def out_row(q):
-                return 4 * k + 2 * dirn + q // 4
+                return 4 * k + 2 * dirn + q // (CHUNKS // 2)
 
             def out_here(q):
                 return (z == c) & (out_row(q) == row)
 
             def out_copy(h, q, ring):
-                return remote(sums.at[dirn, ring], out_place(h, q), r_send.at[dirn, ring], o_recv.at[h, q % 4],
+                return remote(sums.at[dirn, ring], out_place(h, q), r_send.at[dirn, ring], o_recv.at[h, q % (CHUNKS // 2)],
                               (c, out_row(q)))
 
             def share_copy(h, par, q, ring, cc):
@@ -307,6 +320,13 @@
                     a_copy(dirn, q).wait()
                 prod = jnp.dot(a_v[rows, :], xbuf[h, par], preferred_element_type=jnp.float32)
                 sums[dirn, ring] = prod * DAMPING
+
+                part = 2 * dirn + q // (CHUNKS // 2)
+
+                @pl.when(holds_v & (n < 2) & (q % (CHUNKS // 2) == 0) & (4 * k + part != row))
+                def _():
+                    place = vbuf.at[h, pl.ds(part * piece, piece)]
+                    remote(place, place, v_send.at[0], v_recv.at[h, part], (z, row)).wait_recv()
 
                 @pl.when(holds_v)
                 def _():
@@ -364,14 +384,19 @@
                 def _():
                     @pl.when(out_here(q))
                     def _():
-                        out_ref[pl.ds((q % 4) * ch, ch), pl.ds(pl.multiple_of(h * lanes, lanes), lanes)] = sums[dirn, ring]
+                        out_ref[pl.ds((q % (CHUNKS // 2)) * ch, ch), pl.ds(pl.multiple_of(h * lanes, lanes), lanes)] = sums[dirn, ring]
 
                     @pl.when(jnp.logical_not(out_here(q)))
                     def _():
                         out_copy(h, q, ring).start()
 
-        @pl.when(t == 1)
+        @pl.when(t == PERIOD - 3)
         def _():
+            x0_forward(1)
+
+        @pl.when(t == PERIOD - 1)
+        def _():
+            x0_finish(1)
             for h in range(2):
                 s_wait_send(h)
 
@@ -402,7 +427,7 @@
     @pl.when(jnp.logical_not(made_here))
     def _():
         for h in range(2):
-            for q in range(4):
+            for q in range(CHUNKS // 2):
                 place = out_ref.at[pl.ds(q * ch, ch), pl.ds(h * lanes, lanes)]
                 remote(place, place, d_send, o_recv.at[h, q], (z, row)).wait_recv()
 
@@ -452,7 +477,7 @@
                 dma((2, 4)),
                 dma((2, 3)),
                 dma((2, 3)),
-                dma((2, 4)),
+                dma((2, CHUNKS // 2)),
             ],
             compiler_params=pltpu.CompilerParams(collective_id=0, has_side_effects=True,
                                                  vmem_limit_bytes=64 * 1024 * 1024 - 65536),

time: 789 us -> 521 us (0.66)
  Pallas kernels: 785 us -> 518 us
    pallas_call x1, Pallas kernels: 785 us -> 518 us  [local_sweeps(): pl.pallas_call(functools.partial(kernel, block_rows, lanes), name='sweeps...]
where the time goes in v2:
time: 521 us
  Pallas kernels  518 us (99%)
    pallas_call x1, Pallas kernels, local_sweeps(): pl.pallas_call(functools.partial(kernel, block_rows, lanes), name='sweeps...  518 us

profile of v2, /device:TPU:0, one launch (start us, length us, event | category | flops | bytes accessed | tf_op | source)
XLA Modules:
  0.0 521.1 jit_solution(12456373496960789813)
XLA Ops:
  0.0 0.7 convert_element_type.3
  0.7 0.8 broadcast_in_dim.2.d_ref
  1.5 517.5 %sweeps.1 = f32[768,256]{1,0:T(8,128)} custom-call(bf16[3072,6144]{1,0:T(8,128)(2,1)} %a_hbm.1, f32[768,256]{1,0:T(8,128)} %x_ref.1, f32[768,256]{1,0:T(8,128)} %v_ref.1, bf16[768,128]{1,0:T(8,128)(2,1)} %broadcast_in_dim.2.d_ref), custom_call_target="tpu_custom_call" | custom-call | tf_op jit(solution)/shard_map/sweeps/pallas_call | solution.py:443
  519.1 2.1 copy.6

commit v3 on v2

--- a/solution.py
+++ b/solution.py
@@ -14,17 +14,20 @@
 CHUNKS = 12
 PERIOD = 12
 HOP = 2
-GATHER = 4
+SPREAD = 3
+GATHER = 5
 FORWARD = 6
 READY = 7
 RING = 4
+ORDER = 'GPWSUFD'
 PASSES = 2 * SWEEPS
 
 
 def kernel(block_rows, lanes, a_hbm, x_ref, v_ref, d_ref, out_ref,
            a_v, xbuf, rbuf, sums, xs, vbuf, dbuf, sacc, sstage, sbuf, coef,
            a_sem, r_send, r_recv, z_send, z_recv, g_send, g_recv, f_send, f_recv,
-           s_send, s_recv, v_send, v_recv, d_send, d_recv, x0_send, x0_recv, x1_send, x1_recv, o_recv):
+           s_send, s_recv, v_send, v_recv, d_send, d_recv, x0_send, x0_recv, x1_send, x1_recv, o_recv,
+           tbuf, obuf, t_send, t_recv):
     z = lax.axis_index('col')
     row = lax.axis_index('row')
     k = row % 2
@@ -109,9 +112,10 @@
     v_dev = z * 2 + row // 4
     v_self = v_dev == row
 
-    def v_copy(h):
-        return remote(v_ref.at[:, pl.ds(h * lanes, lanes)], vbuf.at[h, pl.ds((row % 4) * piece, piece)],
-                      v_send.at[h], v_recv.at[h, row % 4], (z, v_dev))
+    def v_copy(h, m):
+        return remote(v_ref.at[pl.ds(m * ch, ch), pl.ds(pl.multiple_of(h * lanes, lanes), lanes)],
+                      vbuf.at[h, pl.ds((row % 4) * piece + m * ch, ch)],
+                      v_send.at[h, m], v_recv.at[h, row % 4, m], (z, v_dev))
 
     @pl.when(v_self)
     def _():
@@ -132,27 +136,18 @@
         for m in range(4):
             x0_copy(h, m).start()
 
-    def v_start(h):
-        @pl.when(jnp.logical_not(v_self))
-        def _():
-            v_copy(h).start()
-
     x0_start(0)
-
-    @pl.when(k == 0)
-    def _():
-        v_start(0)
-        x0_start(1)
-
-    @pl.when(k == 1)
-    def _():
-        x0_start(1)
-        v_start(0)
-    v_start(1)
 
     @pl.when(jnp.logical_not(d_self))
     def _():
         d_copy.start()
+
+    @pl.when((k == 0) & jnp.logical_not(v_self))
+    def _():
+        for m in range(CHUNKS // 2):
+            v_copy(0, m).start()
+    x0_start(1)
+
 
     def x0_forward(h):
         for m in range(3):
@@ -189,6 +184,13 @@
             rows = x_rows(h, 1 - par, k * block_rows + dirn * half + q * ch, ch)
             return remote(rows, rows, f_send.at[ring, dirn], f_recv.at[h, dirn, q], (z, partner))
 
+        def out_row(dirn, q):
+            return 4 * k + 2 * dirn + q // (CHUNKS // 2)
+
+        def out_place(h, q, cc):
+            rows = pl.ds((q % (CHUNKS // 2)) * ch + cc * sub, sub)
+            return out_ref.at[rows, pl.ds(pl.multiple_of(h * lanes, lanes), lanes)]
+
         def forward(dirn):
             step = t - 3 * HOP - FORWARD
             old, n, q, h, par = index(step - RING)
@@ -211,6 +213,52 @@
             @pl.when(valid & (n < PASSES - 2))
             def _():
                 forward_copy(h, par, dirn, q, step % RING).wait_recv()
+
+        def spread(dirn):
+            def spread_copy(h, par, q, ring, src):
+                rows = x_rows(h, 1 - par, k * block_rows + dirn * half + q * ch + c * sub, sub)
+                return remote(tbuf.at[h, q, src], rows, t_send.at[ring, src], z_recv.at[h, dirn, q], (src, row))
+
+            def result_copy(h, q, ring, src):
+                return remote(obuf.at[h, q, src], out_place(h, q, c), t_send.at[ring, src],
+                              o_recv.at[h, q % (CHUNKS // 2), c], (src, out_row(dirn, q)))
+
+            step = t - 3 * HOP - SPREAD
+            old, n, q, h, par = index(step - RING)
+            at_end = z == 3 * dirn
+
+            @pl.when(old & at_end & (n < PASSES - 2))
+            def _():
+                for src in range(4):
+                    @pl.when((src != c) & (src != z))
+                    def _():
+                        spread_copy(h, par, q, (step - RING) % RING, src).wait_send()
+
+            @pl.when(old & at_end & (n >= PASSES - 2))
+            def _():
+                for src in range(4):
+                    @pl.when((src != c) & (src != z))
+                    def _():
+                        result_copy(h, q, (step - RING) % RING, src).wait_send()
+            valid, n, q, h, par = index(step)
+
+            @pl.when(valid & at_end & (n < PASSES - 2))
+            def _():
+                for src in range(4):
+                    @pl.when((src != c) & (src != z))
+                    def _():
+                        remote(tbuf.at[h, q, src], tbuf.at[h, q, src], t_send.at[0, 0], t_recv.at[h, q, src],
+                               (z, row)).wait_recv()
+                        spread_copy(h, par, q, step % RING, src).start()
+
+            @pl.when(valid & at_end & (n >= PASSES - 2))
+            def _():
+                for src in range(4):
+                    @pl.when((src != c) & (src != z))
+                    def _():
+                        remote(obuf.at[h, q, src], obuf.at[h, q, src], t_send.at[0, 0], t_recv.at[h, q, src],
+                               (z, row)).wait_recv()
+                        result_copy(h, q, step % RING, src).start()
 
         def gather(dirn):
             step = t - 3 * HOP - GATHER
@@ -265,24 +313,39 @@
                 return remote(sums.at[dirn, ring], rbuf.at[dirn, h, q], r_send.at[dirn, ring], r_recv.at[dirn, h, q],
                               (after, row))
 
-            def out_place(h, q):
-                rows = pl.ds((q % (CHUNKS // 2)) * ch, ch)
-                return out_ref.at[rows, pl.ds(pl.multiple_of(h * lanes, lanes), lanes)]
-
-            def out_row(q):
-                return 4 * k + 2 * dirn + q // (CHUNKS // 2)
-
             def out_here(q):
-                return (z == c) & (out_row(q) == row)
-
-            def out_copy(h, q, ring):
-                return remote(sums.at[dirn, ring], out_place(h, q), r_send.at[dirn, ring], o_recv.at[h, q % (CHUNKS // 2)],
-                              (c, out_row(q)))
-
-            def share_copy(h, par, q, ring, cc):
-                rows = x_rows(h, 1 - par, k * block_rows + dirn * half + q * ch + cc * sub, sub)
-                return remote(xs.at[ring, pl.ds(cc * sub, sub)], rows, z_send.at[ring, cc], z_recv.at[h, dirn, q],
-                              (c, 2 * cc + k))
+                return (z == c) & (out_row(dirn, q) == row)
+
+            def out_copies(h, q, ring, cc, act):
+                mine = sums.at[dirn, ring, pl.ds(cc * sub, sub)]
+
+                @pl.when(((cc == c) | (z == c)) & jnp.logical_not(out_here(q)))
+                def _():
+                    act(remote(mine, out_place(h, q, cc), z_send.at[ring, cc], o_recv.at[h, q % (CHUNKS // 2), cc],
+                               (c, out_row(dirn, q))))
+
+                @pl.when((cc != c) & (z != c))
+                def _():
+                    act(remote(mine, obuf.at[h, q, c], z_send.at[ring, cc], t_recv.at[h, q, c], (z, 2 * cc + k)))
+
+            def share_rows(h, par, q, cc):
+                return x_rows(h, 1 - par, k * block_rows + dirn * half + q * ch + cc * sub, sub)
+
+            def share_copies(h, par, q, ring, cc, act):
+                mine = xs.at[ring, pl.ds(cc * sub, sub)]
+
+                @pl.when((cc == c) & (z != c))
+                def _():
+                    act(remote(mine, share_rows(h, par, q, cc), z_send.at[ring, cc], z_recv.at[h, dirn, q], (c, row)))
+
+                @pl.when((cc != c) & (z == c))
+                def _():
+                    act(remote(mine, share_rows(h, par, q, cc), z_send.at[ring, cc], z_recv.at[h, dirn, q],
+                               (z, 2 * cc + k)))
+
+                @pl.when((cc != c) & (z != c))
+                def _():
+                    act(remote(mine, tbuf.at[h, q, c], z_send.at[ring, cc], t_recv.at[h, q, c], (z, 2 * cc + k)))
 
             step = t - HOP * pos
             old, n, q, h, par = index(step - RING)
@@ -295,17 +358,16 @@
             @pl.when(old & owner & (n < PASSES - 2))
             def _():
                 for cc in range(4):
-                    @pl.when(jnp.logical_not((z == c) & (cc == c)))
-                    def _():
-                        share_copy(h, par, q, ring, cc).wait_send()
+                    share_copies(h, par, q, ring, cc, lambda copy: copy.wait_send())
 
                 @pl.when(q == CHUNKS - 1)
                 def _():
                     s_wait_send(h)
 
-            @pl.when(old & owner & (n >= PASSES - 2) & jnp.logical_not(out_here(q)))
-            def _():
-                out_copy(h, q, ring).wait_send()
+            @pl.when(old & owner & (n >= PASSES - 2))
+            def _():
+                for cc in range(4):
+                    out_copies(h, q, ring, cc, lambda copy: copy.wait_send())
 
             valid, n, q, h, par = index(step)
             ring = step % RING
@@ -323,10 +385,10 @@
 
                 part = 2 * dirn + q // (CHUNKS // 2)
 
-                @pl.when(holds_v & (n < 2) & (q % (CHUNKS // 2) == 0) & (4 * k + part != row))
-                def _():
-                    place = vbuf.at[h, pl.ds(part * piece, piece)]
-                    remote(place, place, v_send.at[0], v_recv.at[h, part], (z, row)).wait_recv()
+                @pl.when(holds_v & (n < 2) & (4 * k + part != row))
+                def _():
+                    place = vbuf.at[h, rows]
+                    remote(place, place, v_send.at[0, 0], v_recv.at[h, part, q % (CHUNKS // 2)], (z, row)).wait_recv()
 
                 @pl.when(holds_v)
                 def _():
@@ -363,9 +425,7 @@
                             place = pl.ds(k * block_rows + start + cc * sub, sub)
                             xbuf[h, 1 - par, place, :] = low[cc * sub:(cc + 1) * sub]
 
-                        @pl.when(jnp.logical_not(here))
-                        def _():
-                            share_copy(h, par, q, ring, cc).start()
+                        share_copies(h, par, q, ring, cc, lambda copy: copy.start())
 
                     @pl.when(q == 0)
                     def _():
@@ -386,9 +446,8 @@
                     def _():
                         out_ref[pl.ds((q % (CHUNKS // 2)) * ch, ch), pl.ds(pl.multiple_of(h * lanes, lanes), lanes)] = sums[dirn, ring]
 
-                    @pl.when(jnp.logical_not(out_here(q)))
-                    def _():
-                        out_copy(h, q, ring).start()
+                    for cc in range(4):
+                        out_copies(h, q, ring, cc, lambda copy: copy.start())
 
         @pl.when(t == PERIOD - 3)
         def _():
@@ -400,24 +459,32 @@
             for h in range(2):
                 s_wait_send(h)
 
-            @pl.when(jnp.logical_not(v_self))
-            def _():
-                for h in range(2):
-                    v_copy(h).wait_send()
 
             @pl.when(jnp.logical_not(d_self))
             def _():
                 d_copy.wait_send()
 
-        for dirn in range(2):
-            forward(dirn)
-        for dirn in range(2):
-            ready(dirn)
-        dangling_term()
-        reduce(1)
-        for dirn in range(2):
-            gather(dirn)
-        reduce(0)
+        turn = t + (1 - k) * (CHUNKS // 2)
+        turn_h = turn // PERIOD
+        turn_m = turn % PERIOD
+
+        @pl.when((turn < 2 * PERIOD) & (turn_m < CHUNKS // 2) & jnp.logical_not(v_self))
+        def _():
+            v_copy(turn_h, turn_m).start()
+
+        @pl.when((t == 2 * PERIOD) & jnp.logical_not(v_self))
+        def _():
+            for h in range(2):
+                for m in range(CHUNKS // 2):
+                    v_copy(h, m).wait_send()
+
+        def both(stage):
+            for dirn in range(2):
+                stage(dirn)
+        stages = {'F': lambda: both(forward), 'W': lambda: both(ready), 'S': dangling_term, 'U': lambda: reduce(1),
+                  'G': lambda: both(gather), 'P': lambda: both(spread), 'D': lambda: reduce(0)}
+        for name in ORDER:
+            stages[name]()
         return carry
 
     lax.fori_loop(0, PASSES * PERIOD + 3 * HOP + FORWARD + RING, slot, 0)
@@ -428,8 +495,9 @@
     def _():
         for h in range(2):
             for q in range(CHUNKS // 2):
-                place = out_ref.at[pl.ds(q * ch, ch), pl.ds(h * lanes, lanes)]
-                remote(place, place, d_send, o_recv.at[h, q], (z, row)).wait_recv()
+                for cc in range(4):
+                    place = out_ref.at[pl.ds(q * ch + cc * sub, sub), pl.ds(h * lanes, lanes)]
+                    remote(place, place, d_send, o_recv.at[h, q, cc], (z, row)).wait_recv()
 
 
 def solution(mesh):
@@ -469,15 +537,19 @@
                 dma((2, 2, CHUNKS)),
                 dma((2, 8)),
                 dma((2, 32)),
-                dma((2,)),
-                dma((2, 4)),
+                dma((2, CHUNKS // 2)),
+                dma((2, 4, CHUNKS // 2)),
                 dma,
                 dma((2,)),
                 dma((2, 4)),
                 dma((2, 4)),
                 dma((2, 3)),
                 dma((2, 3)),
-                dma((2, CHUNKS // 2)),
+                dma((2, CHUNKS // 2, 4)),
+                pltpu.VMEM((2, CHUNKS, 4, ch // 4, lanes), jnp.bfloat16),
+                pltpu.VMEM((2, CHUNKS, 4, ch // 4, lanes), jnp.float32),
+                dma((RING, 4)),
+                dma((2, CHUNKS, 4)),
             ],
             compiler_params=pltpu.CompilerParams(collective_id=0, has_side_effects=True,
                                                  vmem_limit_bytes=64 * 1024 * 1024 - 65536),

time: 521 us -> 488 us (0.937)
  Pallas kernels: 518 us -> 484 us
    pallas_call x1, Pallas kernels: 518 us -> 484 us  [local_sweeps(): pl.pallas_call(functools.partial(kernel, block_rows, lanes), name='sweeps...]
where the time goes in v3:
time: 488 us
  Pallas kernels  484 us (99%)
    pallas_call x1, Pallas kernels, local_sweeps(): pl.pallas_call(functools.partial(kernel, block_rows, lanes), name='sweeps...  484 us

profile of v3, /device:TPU:0, one launch (start us, length us, event | category | flops | bytes accessed | tf_op | source)
XLA Modules:
  0.0 487.8 jit_solution(4341913449958429627)
XLA Ops:
  0.0 0.7 convert_element_type.3
  0.7 0.8 broadcast_in_dim.2.d_ref
  1.5 484.2 %sweeps.1 = f32[768,256]{1,0:T(8,128)} custom-call(bf16[3072,6144]{1,0:T(8,128)(2,1)} %a_hbm.1, f32[768,256]{1,0:T(8,128)} %x_ref.1, f32[768,256]{1,0:T(8,128)} %v_ref.1, bf16[768,128]{1,0:T(8,128)(2,1)} %broadcast_in_dim.2.d_ref), custom_call_target="tpu_custom_call" | custom-call | tf_op jit(solution)/shard_map/sweeps/pallas_call | solution.py:511
  485.8 2.1 copy.6

commit v4 on v3

--- a/solution.py
+++ b/solution.py
@@ -19,6 +19,7 @@
 FORWARD = 6
 READY = 7
 RING = 4
+RELAY = 3
 ORDER = 'GPWSUFD'
 PASSES = 2 * SWEEPS
 
@@ -27,7 +28,7 @@
            a_v, xbuf, rbuf, sums, xs, vbuf, dbuf, sacc, sstage, sbuf, coef,
            a_sem, r_send, r_recv, z_send, z_recv, g_send, g_recv, f_send, f_recv,
            s_send, s_recv, v_send, v_recv, d_send, d_recv, x0_send, x0_recv, x1_send, x1_recv, o_recv,
-           tbuf, obuf, t_send, t_recv):
+           tbuf, obuf, t_send, t_recv, vstage, w_send, w_recv):
     z = lax.axis_index('col')
     row = lax.axis_index('row')
     k = row % 2
@@ -117,6 +118,19 @@
                       vbuf.at[h, pl.ds((row % 4) * piece + m * ch, ch)],
                       v_send.at[h, m], v_recv.at[h, row % 4, m], (z, v_dev))
 
+    far_row = 2 * (3 - z) + 1
+    near_row = 2 * ((z // 2) * 2 + 1 - z % 2) + 1
+    is_far = row == far_row
+    is_relay = row == near_row
+
+    def far_copy(h, m):
+        return remote(v_ref.at[pl.ds(m * ch, ch), pl.ds(pl.multiple_of(h * lanes, lanes), lanes)],
+                      vstage.at[h, pl.ds(m * ch, ch)], v_send.at[h, m], w_recv.at[h, m], (z, near_row))
+
+    def relay_copy(h, m):
+        return remote(vstage.at[h, pl.ds(m * ch, ch)], vbuf.at[h, pl.ds((far_row % 4) * piece + m * ch, ch)],
+                      w_send.at[h, m], v_recv.at[h, far_row % 4, m], (z, z * 2 + far_row // 4))
+
     @pl.when(v_self)
     def _():
         for h in range(2):
@@ -468,15 +482,34 @@
         turn_h = turn // PERIOD
         turn_m = turn % PERIOD
 
-        @pl.when((turn < 2 * PERIOD) & (turn_m < CHUNKS // 2) & jnp.logical_not(v_self))
+        sends_v = (turn < 2 * PERIOD) & (turn_m < CHUNKS // 2) & jnp.logical_not(v_self)
+
+        @pl.when(sends_v & jnp.logical_not(is_far))
         def _():
             v_copy(turn_h, turn_m).start()
+
+        @pl.when(sends_v & is_far)
+        def _():
+            far_copy(turn_h, turn_m).start()
+
+        past = t - RELAY
+
+        @pl.when((past >= 0) & (past < 2 * PERIOD) & (past % PERIOD < CHUNKS // 2) & is_relay)
+        def _():
+            far_copy(past // PERIOD, past % PERIOD).wait_recv()
+            relay_copy(past // PERIOD, past % PERIOD).start()
 
         @pl.when((t == 2 * PERIOD) & jnp.logical_not(v_self))
         def _():
             for h in range(2):
                 for m in range(CHUNKS // 2):
                     v_copy(h, m).wait_send()
+
+        @pl.when((t == 2 * PERIOD) & is_relay)
+        def _():
+            for h in range(2):
+                for m in range(CHUNKS // 2):
+                    relay_copy(h, m).wait_send()
 
         def both(stage):
             for dirn in range(2):
@@ -550,6 +583,9 @@
                 pltpu.VMEM((2, CHUNKS, 4, ch // 4, lanes), jnp.float32),
                 dma((RING, 4)),
                 dma((2, CHUNKS, 4)),
+                pltpu.VMEM((2, piece, lanes), jnp.float32),
+                dma((2, CHUNKS // 2)),
+                dma((2, CHUNKS // 2)),
             ],
             compiler_params=pltpu.CompilerParams(collective_id=0, has_side_effects=True,
                                                  vmem_limit_bytes=64 * 1024 * 1024 - 65536),

time: 488 us -> 485 us (level)
  no operation moved by 1% of the time
where the time goes in v4:
time: 485 us
  Pallas kernels  481 us (99%)
    pallas_call x1, Pallas kernels, local_sweeps(): pl.pallas_call(functools.partial(kernel, block_rows, lanes), name='sweeps...  481 us

profile of v4, /device:TPU:0, one launch (start us, length us, event | category | flops | bytes accessed | tf_op | source)
XLA Modules:
  0.0 485.0 jit_solution(12318048502358141065)
XLA Ops:
  0.0 0.7 convert_element_type.3
  0.7 0.8 broadcast_in_dim.2.d_ref
  1.5 481.4 %sweeps.1 = f32[768,256]{1,0:T(8,128)} custom-call(bf16[3072,6144]{1,0:T(8,128)(2,1)} %a_hbm.1, f32[768,256]{1,0:T(8,128)} %x_ref.1, f32[768,256]{1,0:T(8,128)} %v_ref.1, bf16[768,128]{1,0:T(8,128)(2,1)} %broadcast_in_dim.2.d_ref), custom_call_target="tpu_custom_call" | custom-call | tf_op jit(solution)/shard_map/sweeps/pallas_call | solution.py:544
  482.9 2.1 copy.6
